TPU v7x, 32 devices: a whole 2x2x4 slice. The times are simulated.
32 devices in a mesh: dp: 16 (over z, x, core), tensor: 2 (over y).
Axes of the slice: x: 2, y: 2, z: 4, core: 2. Of those that a mesh axis runs over, the one named last changes fastest.
Arguments:
- inputs: bfloat16 [16384, 768], P(('dp', 'tensor')), may hold values from -6 to 6
- lengths: int32 [16], P('dp'), may hold values from 512 to 1024, as said below
- query_weight: bfloat16 [768, 768], P(None, 'tensor'), may hold values from -0.21875 to 0.21875
- query_bias: float32 [768], P('tensor'), may hold values from -3 to 3
- key_weight: bfloat16 [768, 768], P(None, 'tensor'), may hold values from -0.21875 to 0.21875
- value_weight: bfloat16 [768, 768], P(None, 'tensor'), may hold values from -0.21875 to 0.21875
- value_bias: float32 [768], P('tensor'), may hold values from -3 to 3
- proj_weight: bfloat16 [768, 768], P('tensor'), may hold values from -4 to 4
- proj_bias: float32 [768], replicated, may hold values from -3 to 3
- attn_gain: float32 [768], replicated, may hold values from 0.1 to 1.9
- attn_shift: float32 [768], replicated, may hold values from -2 to 2
- up_weight: bfloat16 [768, 3072], P(None, 'tensor'), may hold values from -0.21875 to 0.21875
- up_bias: float32 [3072], P('tensor'), may hold values from -3 to 3
- down_weight: bfloat16 [3072, 768], P('tensor'), may hold values from -0.109375 to 0.109375
- down_bias: float32 [768], replicated, may hold values from -3 to 3
- ffn_gain: float32 [768], replicated, may hold values from 0.1 to 1.9
- ffn_shift: float32 [768], replicated, may hold values from -2 to 2
- filter_couple_scores: float32 [12, 512, 512], P('tensor', 'dp'), may hold values from -5 to 5
- filter_smoothing_jitter: float32 [12, 512, 512], P('tensor', 'dp'), may hold values from -5 to 5
- cotangent: bfloat16 [16384, 768], P(('dp', 'tensor')), may hold values from -6 to 6
Outputs:
- layer_output: bfloat16 [16384, 768], P(('dp', 'tensor'))
- input_grads: bfloat16 [16384, 768], P(('dp', 'tensor'))
- query_grads: float32 [768, 768], P(None, 'tensor')
- key_grads: float32 [768, 768], P(None, 'tensor')
- value_grads: float32 [768, 768], P(None, 'tensor')
- proj_grads: float32 [768, 768], P('tensor')
- up_grads: float32 [768, 3072], P(None, 'tensor')
- down_grads: float32 [3072, 768], P('tensor')
- query_bias_grads: float32 [768], P('tensor')
- value_bias_grads: float32 [768], P('tensor')
- up_bias_grads: float32 [3072], P('tensor')
- proj_bias_grads: float32 [768], replicated
- down_bias_grads: float32 [768], replicated
- attn_gain_grads: float32 [768], replicated
- attn_shift_grads: float32 [768], replicated
- ffn_gain_grads: float32 [768], replicated
- ffn_shift_grads: float32 [768], replicated
- mask_logit_gradients: float32 [12, 512, 512], P('tensor', 'dp')
Inputs may be any that keep to these rules, and one draw needn't show every extreme that they name: Each sequence's live slots are its first lengths[b]; at least one sequence fills all 1024 slots.
All inputs are finite; a program needn't handle non-finite values.
Results may differ from a plain program's by a relative error of at most 0.015.
Values may be sent and summed in bfloat16 or wider, within the bound.
A program may use at most 192 MiB of HBM per device.

v0:
```python
import math

import jax
import jax.numpy as jnp
from jax import lax
from jax.sharding import PartitionSpec as P

HEAD_DIM = 64


softening_heat = 0.5
epsilon = 1e-05


def layer_norm(values, gain, shift):
    centre = values - jnp.mean(values, axis=-1, keepdims=True)
    spread = jnp.mean(centre * centre, axis=-1, keepdims=True)
    inverse = lax.rsqrt(spread + epsilon)
    normal = centre * inverse
    return (normal * gain + shift, normal, inverse)


def norm_back(upstream, normal, inverse, gain):
    scaled = upstream * gain
    first_mean = jnp.mean(scaled, axis=-1, keepdims=True)
    second_mean = jnp.mean(scaled * normal, axis=-1, keepdims=True)
    grad_in = inverse * (scaled - first_mean - normal * second_mean)
    return (grad_in, jnp.sum(upstream * normal, axis=0), jnp.sum(upstream, axis=0))


def on_device(
    inputs,
    lengths,
    query_weight,
    query_bias,
    key_weight,
    value_weight,
    value_bias,
    proj_weight,
    proj_bias,
    attn_gain,
    attn_shift,
    up_weight,
    up_bias,
    down_weight,
    down_bias,
    ffn_gain,
    ffn_shift,
    filter_couple_scores,
    filter_smoothing_jitter,
    cotangent,
):
    rows_half = inputs.shape[0]
    seq_len = rows_half * lax.axis_size("tensor")
    local_width = query_weight.shape[1]
    local_heads = local_width // HEAD_DIM
    window = filter_couple_scores.shape[2]
    blocks = seq_len // window
    score_scale = 1.0 / math.sqrt(HEAD_DIM)
    slot_ids = jnp.arange(seq_len, dtype=jnp.int32)
    live_slots = slot_ids < lengths[0]
    own_live = lax.dynamic_slice_in_dim(live_slots, lax.axis_index("tensor") * rows_half, rows_half)
    softened_filter = jax.nn.sigmoid(
        (filter_couple_scores + filter_smoothing_jitter) / softening_heat
    )
    trainable_focus_filter = lax.all_gather(
        softened_filter.astype(jnp.bfloat16), "dp", axis=1, tiled=True
    )
    full_rows = lax.all_gather(inputs, "tensor", axis=0, tiled=True)
    joint_weight = jnp.concatenate([query_weight, key_weight, value_weight], axis=1)
    joint = jnp.dot(full_rows, joint_weight, preferred_element_type=jnp.float32)
    queries = (joint[:, :local_width] + query_bias).astype(jnp.bfloat16)
    queries = queries.reshape(seq_len, local_heads, HEAD_DIM)
    key_rows = joint[:, local_width : 2 * local_width].astype(jnp.bfloat16)
    key_rows = key_rows.reshape(seq_len, local_heads, HEAD_DIM)
    value_rows = (joint[:, 2 * local_width :] + value_bias).astype(jnp.bfloat16)
    value_rows = value_rows.reshape(seq_len, local_heads, HEAD_DIM)

    def scores_for(query_block):
        scores = (
            jnp.einsum("qhd,khd->hqk", query_block, key_rows, preferred_element_type=jnp.float32)
            * score_scale
        )
        return jnp.where(live_slots[None, None, :], scores, -1e30)

    def apply_mask(softmax_out):
        tiles = (
            softmax_out.reshape(local_heads, window, blocks, window)
            * trainable_focus_filter[:, :, None, :]
        )
        return tiles.reshape(local_heads, window, seq_len)

    def attend(query_block):
        scores = scores_for(query_block)
        row_max = jnp.max(scores, axis=-1)
        exponent = jnp.exp(scores - row_max[..., None])
        row_total = jnp.sum(exponent, axis=-1)
        weighted = apply_mask(exponent / row_total[..., None]).astype(jnp.bfloat16)
        context = jnp.einsum(
            "hqk,khd->qhd", weighted, value_rows, preferred_element_type=jnp.float32
        )
        return (context.astype(jnp.bfloat16), row_max + jnp.log(row_total))

    query_blocks = queries.reshape(blocks, window, local_heads, HEAD_DIM)
    contexts, log_totals = lax.map(attend, query_blocks)
    heads_out = contexts.reshape(seq_len, local_width)
    piece = heads_out
    attn_half = lax.psum_scatter(
        jnp.dot(piece, proj_weight, preferred_element_type=jnp.float32),
        "tensor",
        scatter_dimension=0,
        tiled=True,
    )
    normed, normal_attn, inverse_attn = layer_norm(
        inputs.astype(jnp.float32) + attn_half + proj_bias, attn_gain, attn_shift
    )
    hidden_rows = lax.all_gather(normed.astype(jnp.bfloat16), "tensor", axis=0, tiled=True)
    upper = jnp.dot(hidden_rows, up_weight, preferred_element_type=jnp.float32) + up_bias
    gelu_out, gelu_pull = jax.vjp(lambda given: jax.nn.gelu(given, approximate=False), upper)
    active = gelu_out.astype(jnp.bfloat16)
    piece = active
    ffn_half = lax.psum_scatter(
        jnp.dot(piece, down_weight, preferred_element_type=jnp.float32),
        "tensor",
        scatter_dimension=0,
        tiled=True,
    )
    result, normal_ffn, inverse_ffn = layer_norm(normed + ffn_half + down_bias, ffn_gain, ffn_shift)
    layer_output = result.astype(jnp.bfloat16)
    grad_out = cotangent.astype(jnp.float32) * own_live[:, None].astype(jnp.float32)
    grad_ffn, ffn_gain_grad, ffn_shift_grad = norm_back(grad_out, normal_ffn, inverse_ffn, ffn_gain)
    down_bias_grad = jnp.sum(grad_ffn, axis=0)
    grad_ffn_rows = lax.all_gather(grad_ffn.astype(jnp.bfloat16), "tensor", axis=0, tiled=True)
    down_weight_grad = jnp.einsum(
        "sf,sd->fd", active, grad_ffn_rows, preferred_element_type=jnp.float32
    )
    grad_active = jnp.einsum(
        "sd,fd->sf", grad_ffn_rows, down_weight, preferred_element_type=jnp.float32
    )
    grad_upper = gelu_pull(grad_active)[0].astype(jnp.bfloat16)
    up_bias_grad = jnp.sum(grad_upper, axis=0, dtype=jnp.float32)
    up_weight_grad = jnp.einsum(
        "sd,sf->df", hidden_rows, grad_upper, preferred_element_type=jnp.float32
    )
    piece = grad_upper
    grad_hidden = lax.psum_scatter(
        jnp.einsum("sf,df->sd", piece, up_weight, preferred_element_type=jnp.float32),
        "tensor",
        scatter_dimension=0,
        tiled=True,
    )
    grad_attn, attn_gain_grad, attn_shift_grad = norm_back(
        grad_ffn + grad_hidden, normal_attn, inverse_attn, attn_gain
    )
    proj_bias_grad = jnp.sum(grad_attn, axis=0)
    grad_attn_rows = lax.all_gather(grad_attn.astype(jnp.bfloat16), "tensor", axis=0, tiled=True)
    proj_weight_grad = jnp.einsum(
        "sk,sd->kd", heads_out, grad_attn_rows, preferred_element_type=jnp.float32
    )
    grad_context = jnp.einsum(
        "sd,kd->sk", grad_attn_rows, proj_weight, preferred_element_type=jnp.float32
    ).astype(jnp.bfloat16)

    def attend_back(carry, pieces):
        key_total, value_total, mask_total = carry
        query_block, grad_block, log_block = pieces
        softmax_out = jnp.exp(scores_for(query_block) - log_block[..., None])
        weighted = apply_mask(softmax_out)
        grad_weighted = jnp.einsum(
            "qhd,khd->hqk", grad_block, value_rows, preferred_element_type=jnp.float32
        )
        value_total = value_total + jnp.einsum(
            "hqk,qhd->khd",
            weighted.astype(jnp.bfloat16),
            grad_block,
            preferred_element_type=jnp.float32,
        )
        grad_tiles = grad_weighted.reshape(local_heads, window, blocks, window)
        mask_total = mask_total + jnp.sum(
            grad_tiles * softmax_out.reshape(local_heads, window, blocks, window), axis=2
        )
        grad_softmax = (grad_tiles * trainable_focus_filter[:, :, None, :]).reshape(
            local_heads, window, seq_len
        )
        inner = jnp.sum(grad_weighted * weighted, axis=-1, keepdims=True)
        grad_scores = (softmax_out * (grad_softmax - inner) * score_scale).astype(jnp.bfloat16)
        query_grad = jnp.einsum(
            "hqk,khd->qhd", grad_scores, key_rows, preferred_element_type=jnp.float32
        )
        key_total = key_total + jnp.einsum(
            "hqk,qhd->khd", grad_scores, query_block, preferred_element_type=jnp.float32
        )
        return ((key_total, value_total, mask_total), query_grad.astype(jnp.bfloat16))

    zero_rows = jnp.zeros((seq_len, local_heads, HEAD_DIM), jnp.float32)
    zero_mask = jnp.zeros((local_heads, window, window), jnp.float32)
    (key_total, value_total, mask_total), query_grads = lax.scan(
        attend_back,
        (zero_rows, zero_rows, zero_mask),
        (query_blocks, grad_context.reshape(blocks, window, local_heads, HEAD_DIM), log_totals),
    )
    joint_grad = jnp.concatenate(
        [
            query_grads.reshape(seq_len, local_width),
            key_total.astype(jnp.bfloat16).reshape(seq_len, local_width),
            value_total.astype(jnp.bfloat16).reshape(seq_len, local_width),
        ],
        axis=1,
    )
    joint_weight_grad = jnp.einsum(
        "sd,sk->dk", full_rows, joint_grad, preferred_element_type=jnp.float32
    )
    query_weight_grad = joint_weight_grad[:, :local_width]
    key_weight_grad = joint_weight_grad[:, local_width : 2 * local_width]
    value_weight_grad = joint_weight_grad[:, 2 * local_width :]
    query_bias_grad = jnp.sum(joint_grad[:, :local_width], axis=0, dtype=jnp.float32)
    value_bias_grad = jnp.sum(joint_grad[:, 2 * local_width :], axis=0, dtype=jnp.float32)
    piece = joint_grad
    grad_inputs = lax.psum_scatter(
        jnp.einsum("sk,dk->sd", piece, joint_weight, preferred_element_type=jnp.float32).astype(
            jnp.bfloat16
        ),
        "tensor",
        scatter_dimension=0,
        tiled=True,
    ).astype(jnp.float32)
    input_grads = (grad_attn + grad_inputs).astype(jnp.bfloat16)
    filter_slope_lines = lax.psum_scatter(mask_total, "dp", scatter_dimension=1, tiled=True)
    mask_logit_gradients = (
        filter_slope_lines * softened_filter * (1.0 - softened_filter) / softening_heat
    )
    (
        query_weight_grad,
        key_weight_grad,
        value_weight_grad,
        proj_weight_grad,
        query_bias_grad,
        value_bias_grad,
        up_weight_grad,
        down_weight_grad,
        up_bias_grad,
    ) = lax.psum(
        (
            query_weight_grad,
            key_weight_grad,
            value_weight_grad,
            proj_weight_grad,
            query_bias_grad,
            value_bias_grad,
            up_weight_grad,
            down_weight_grad,
            up_bias_grad,
        ),
        "dp",
    )
    (
        proj_bias_grad,
        down_bias_grad,
        attn_gain_grad,
        attn_shift_grad,
        ffn_gain_grad,
        ffn_shift_grad,
    ) = lax.psum(
        (
            proj_bias_grad,
            down_bias_grad,
            attn_gain_grad,
            attn_shift_grad,
            ffn_gain_grad,
            ffn_shift_grad,
        ),
        ("dp", "tensor"),
    )
    return (
        layer_output,
        input_grads,
        query_weight_grad,
        key_weight_grad,
        value_weight_grad,
        proj_weight_grad,
        up_weight_grad,
        down_weight_grad,
        query_bias_grad,
        value_bias_grad,
        up_bias_grad,
        proj_bias_grad,
        down_bias_grad,
        attn_gain_grad,
        attn_shift_grad,
        ffn_gain_grad,
        ffn_shift_grad,
        mask_logit_gradients,
    )


def solution(mesh):
    in_specs = (
        P(("dp", "tensor"), None),
        P("dp"),
        P(None, "tensor"),
        P("tensor"),
        P(None, "tensor"),
        P(None, "tensor"),
        P("tensor"),
        P("tensor", None),
        P(),
        P(),
        P(),
        P(None, "tensor"),
        P("tensor"),
        P("tensor", None),
        P(),
        P(),
        P(),
        P("tensor", "dp", None),
        P("tensor", "dp", None),
        P(("dp", "tensor"), None),
    )
    out_specs = (
        P(("dp", "tensor"), None),
        P(("dp", "tensor"), None),
        P(None, "tensor"),
        P(None, "tensor"),
        P(None, "tensor"),
        P("tensor", None),
        P(None, "tensor"),
        P("tensor", None),
        P("tensor"),
        P("tensor"),
        P("tensor"),
        P(),
        P(),
        P(),
        P(),
        P(),
        P(),
        P("tensor", "dp", None),
    )
    return jax.shard_map(
        on_device, mesh=mesh, in_specs=in_specs, out_specs=out_specs, check_vma=False
    )
```

profile of v0, /device:TPU:0, one launch (start us, length us, event | category | flops | bytes accessed | tf_op | source)
XLA Modules:
  0.0 1162.9 jit_solution(14874265997577795067)
XLA Ops:
  14.8 24.7 %all-gather.6.cloned.1.call-done = bf16[1024,768]{1,0:T(8,128)(2,1)} async-done(((bf16[512,768]{1,0:T(8,128)(2,1)}), bf16[1024,768]{1,0:T(8,128)(2,1)}) %all-gather.6.cloned.1.call-update) | async-done | bytes 1572880 | tf_op jit(solution)/shard_map/all_gather | solution.py:69
  50.6 37.2 %all-gather.8.cloned.1.call-done = bf16[6,512,512]{2,1,0:T(8,128)(2,1)} async-done(((bf16[6,32,512]{2,1,0:T(8,128)(2,1)}), bf16[6,512,512]{2,1,0:T(8,128)(2,1)}) %all-gather.8.cloned.1.call-update) | async-done | bytes 3145744 | tf_op jit(solution)/shard_map/all_gather | solution.py:66
  88.8 84.2 %while.30 = (s32[]{:T(128)}, bf16[2,512,6,64]{1,3,2,0:T(8,128)(2,1)}, f32[2,6,512]{2,1,0:T(8,128)S(1)}, bf16[2,512,6,64]{1,3,2,0:T(8,128)(2,1)}, bf16[1024,6,64]...) while((s32[]{:T(128)}, ...), condition=%wide.region_3.4_spmd.clone, body=%wide.region_0.3_spmd.clone.sunk | while | flops 846395392 | bytes 103145664 | solution.py:105
  100.1 17.0 %mul.486 = f32[6,512,1024]{2,1,0:T(8,128)} reshape(f32[6,512,2,512]{3,2,1,0:T(2,128)} %mul.485) | data formatting | bytes 25165824 | tf_op jit(solution)/shard_map/while/body/eval_jaxpr/mul | solution.py:88
  142.2 17.0 %mul.486 = f32[6,512,1024]{2,1,0:T(8,128)} reshape(f32[6,512,2,512]{3,2,1,0:T(2,128)} %mul.485) | data formatting | bytes 25165824 | tf_op jit(solution)/shard_map/while/body/eval_jaxpr/mul | solution.py:88
  179.8 41.9 %reduce-scatter.6.cloned.1.call-done = f32[512,768]{1,0:T(8,128)} async-done(((f32[1024,768]{1,0:T(8,128)}), f32[512,768]{1,0:T(8,128)}) %reduce-scatter.6.cloned.1.call-update) | async-done | bytes 1572880 | tf_op jit(solution)/shard_map/reduce_scatter | solution.py:108
  225.9 27.3 %all-gather.10.cloned.1.call-done = bf16[1024,768]{1,0:T(8,128)(2,1)} async-done(((bf16[512,768]{1,0:T(8,128)(2,1)}), bf16[1024,768]{1,0:T(8,128)(2,1)}) %all-gather.10.cloned.1.call-update) | async-done | bytes 1572880 | tf_op jit(solution)/shard_map/all_gather | solution.py:117
  253.2 18.8 %multiply_convert_fusion.9 = (bf16[1024,1536]{1,0:T(8,128)(2,1)S(1)}, f32[1024,1536]{1,0:T(8,128)}, f32[1024,1536]{1,0:T(8,128)}) fusion(f32[1536]{0:T(1024)S(1)} %copy-done.49, bf16[1024,768]{1,0:T(8,128)(2,1)} %all-gather.10.cloned.1.call-done, bf16[768,1536]{1,0:T(8,128)(2,1)S(1)} %copy-done), kind=kOutput, calls=%fused_computation.61 | convolution fusion | flops 2519728128 | bytes 19666944 | tf_op jit(solution)/shard_map/dot_general | solution.py:118
  278.7 42.8 %reduce-scatter.8.cloned.1.call-done = f32[512,768]{1,0:T(8,128)} async-done(((f32[1024,768]{1,0:T(8,128)}), f32[512,768]{1,0:T(8,128)}) %reduce-scatter.8.cloned.1.call-update) | async-done | bytes 1572880 | tf_op jit(solution)/shard_map/reduce_scatter | solution.py:122
  330.2 27.3 %all-gather.12.cloned.1.call-done = bf16[1024,768]{1,0:T(8,128)(2,1)} async-done(((bf16[512,768]{1,0:T(8,128)(2,1)}), bf16[1024,768]{1,0:T(8,128)(2,1)}) %all-gather.12.cloned.1.call-update) | async-done | bytes 1572880 | tf_op jit(solution)/shard_map/all_gather | solution.py:133
  374.4 43.5 %reduce-scatter.10.cloned.1.call-done = f32[512,768]{1,0:T(8,128)} async-done(((f32[1024,768]{1,0:T(8,128)}), f32[512,768]{1,0:T(8,128)}) %reduce-scatter.10.cloned.1.call-update) | async-done | bytes 1572880 | tf_op jit(solution)/shard_map/reduce_scatter | solution.py:146
  425.0 27.3 %all-gather.14.cloned.1.call-done = bf16[1024,768]{1,0:T(8,128)(2,1)} async-done(((bf16[512,768]{1,0:T(8,128)(2,1)}), bf16[1024,768]{1,0:T(8,128)(2,1)}) %all-gather.14.cloned.1.call-update) | async-done | bytes 1572880 | tf_op jit(solution)/shard_map/all_gather | solution.py:156
  464.3 292.9 %while.31 = (s32[]{:T(128)}, f32[1024,6,64]{0,2,1:T(8,128)}, f32[1024,6,64]{0,2,1:T(8,128)S(1)}, f32[6,512,512]{2,1,0:T(8,128)}, bf16[2,512,6,64]{1,3,2,0:T(8,12...) while((s32[]{:T(128)}, f32[1024,6,64]{0,2,1:T(8,128)}, ...), condition=%wide.region_18.19_spmd.clone, body=%wide.region_15.18_spmd.clone.sunk | while | flops 3740476416 | bytes 352058144 | solution.py:197
  494.8 22.4 %reduce_sum.228 = f32[6,512,512]{2,1,0:T(8,128)} reduce(f32[6,512,2,512]{3,2,1,0:T(2,128)} %mul.507, f32[]{:T(128)} %constant.61.clone.11..sunk), dimensions={2}, to_apply=%region_17.17 | reduce | flops 1572864 | bytes 18874372 | tf_op jit(solution)/shard_map/while/body/eval_jaxpr/reduce_sum | solution.py:179
  549.5 24.8 %fusion.187 = bf16[2,512,6,64]{1,3,2,0:T(8,128)(2,1)} fusion(bf16[2,512,6,64]{1,3,2,0:T(8,128)(2,1)} %get-tuple-element.530, s32[]{:T(128)S(6)} %copy.74, bf16[1024,6,64]{0,2,1:T(8,128)(2,1)S(1)} %get-tuple-element.547, f32[6,512,1024]{2,1,0:T(8,128)} %mul.506, f32[6,512,1024]{2,1,0:T(8,128)} %copy-done.2, ...), kind=kOutput, calls=%fused_computation.34.clone.1 | convolution fusion | flops 1249054720 | bytes 53906944 | tf_op jit(solution)/shard_map/while/body/eval_jaxpr/hqk,khd->qhd/dot_general | solution.py:187
  584.3 25.5 %bitcast_add_fusion.4 = f32[1024,6,64]{0,2,1:T(8,128)} fusion(f32[1024,6,64]{0,2,1:T(8,128)} %get-tuple-element.527, pred[]{:T(512)S(6)} %compare.3, bf16[2,512,6,64]{1,3,2,0:T(8,128)(2,1)S(1)} %get-tuple-element.546, s32[]{:T(128)S(6)} %copy.74, f32[6,512,1024]{2,1,0:T(8,128)} %mul.506, f32[6,512,1024]{2,1,0:T(8,128)} %copy-done.2, ...), kind=kOutput, calls=%fused_computation.30.clone.1 | convolution fusion | flops 1249644544 | bytes 56266752 | tf_op jit(solution)/shard_map/while/body/eval_jaxpr/hqk,qhd->khd/dot_general | solution.py:190
  640.1 22.4 %reduce_sum.228 = f32[6,512,512]{2,1,0:T(8,128)} reduce(f32[6,512,2,512]{3,2,1,0:T(2,128)} %mul.507, f32[]{:T(128)} %constant.61.clone.11..sunk), dimensions={2}, to_apply=%region_17.17 | reduce | flops 1572864 | bytes 18874372 | tf_op jit(solution)/shard_map/while/body/eval_jaxpr/reduce_sum | solution.py:179
  679.6 17.0 %mul.506 = f32[6,512,1024]{2,1,0:T(8,128)} reshape(f32[6,512,2,512]{3,2,1,0:T(2,128)} %mul.505) | data formatting | bytes 25165824 | tf_op jit(solution)/shard_map/while/body/eval_jaxpr/mul | solution.py:182
  696.6 24.7 %fusion.187 = bf16[2,512,6,64]{1,3,2,0:T(8,128)(2,1)} fusion(bf16[2,512,6,64]{1,3,2,0:T(8,128)(2,1)} %get-tuple-element.530, s32[]{:T(128)S(6)} %copy.74, bf16[1024,6,64]{0,2,1:T(8,128)(2,1)S(1)} %get-tuple-element.547, f32[6,512,1024]{2,1,0:T(8,128)} %mul.506, f32[6,512,1024]{2,1,0:T(8,128)} %copy-done.2, ...), kind=kOutput, calls=%fused_computation.34.clone.1 | convolution fusion | flops 1249054720 | bytes 53906944 | tf_op jit(solution)/shard_map/while/body/eval_jaxpr/hqk,khd->qhd/dot_general | solution.py:187
  731.3 25.7 %bitcast_add_fusion.4 = f32[1024,6,64]{0,2,1:T(8,128)} fusion(f32[1024,6,64]{0,2,1:T(8,128)} %get-tuple-element.527, pred[]{:T(512)S(6)} %compare.3, bf16[2,512,6,64]{1,3,2,0:T(8,128)(2,1)S(1)} %get-tuple-element.546, s32[]{:T(128)S(6)} %copy.74, f32[6,512,1024]{2,1,0:T(8,128)} %mul.506, f32[6,512,1024]{2,1,0:T(8,128)} %copy-done.2, ...), kind=kOutput, calls=%fused_computation.30.clone.1 | convolution fusion | flops 1249644544 | bytes 56266752 | tf_op jit(solution)/shard_map/while/body/eval_jaxpr/hqk,qhd->khd/dot_general | solution.py:190
  785.2 40.9 %all-reduce = (f32[768]{0:T(1024)}, f32[768]{0:T(1024)}, f32[768]{0:T(1024)}, f32[768]{0:T(1024)}, f32[768]{0:T(1024)}, /*index=5*/f32[768]{0:T(1024)}) all-reduce(f32[768]{0:T(1024)S(1)} %copy-done.36, f32[768]{0:T(1024)S(1)} %copy-done.35, f32[768]{0:T(1024)S(1)} %copy-done.38, ...), channel_id=1, replica_groups=mesh['dp'=16,'tensor'=2] {'dp','tensor'}, use_global_device_ids=true, to_apply=%region_33.34 | all-reduce | flops 4608 | bytes 36864 | tf_op jit(solution)/shard_map/psum | solution.py:263
  826.5 63.8 %all-reduce.1 = (f32[384]{0:T(512)}, f32[384]{0:T(512)}, f32[1536]{0:T(1024)}) all-reduce(f32[384]{0:T(512)S(1)} %reduce_sum.193, f32[384]{0:T(512)S(1)} %reduce_sum.195, f32[1536]{0:T(1024)S(1)} %copy-done.40), channel_id=1, replica_groups=mesh['dp'=16,'tensor'=2] {'dp'}, use_global_device_ids=true, to_apply=%region_27.28 | all-reduce | flops 2304 | bytes 18432 | tf_op jit(solution)/shard_map/psum | solution.py:242
  892.6 163.7 %all-reduce.5.cloned.1.call-done = (f32[768,384]{0,1:T(8,128)}, f32[768,384]{0,1:T(8,128)}, f32[768,384]{0,1:T(8,128)}, f32[384,768]{1,0:T(8,128)}, f32[768,1536]{1,0:T(8,128)}, /*index=5*/f32[1536,768]{1,0:T(8,128)}) async-done(((f32[768,384]{0,1:T(8,128)}, f32[768,384]{0,1:T(8,128)}, f32[768,384]{0,1:T(8,128)}, f32[384,768]{1,0:T(8,128)}, f32[768,1536]{1,0:T(8,128)}, /*index=5*/f32[1536,768]{1,0:T(8,128)}), ...) | async-done | bytes 14155792 | tf_op jit(solution)/shard_map/psum | solution.py:242
  1063.2 82.3 %reduce-scatter.14.cloned.1.call-done = f32[6,32,512]{2,1,0:T(8,128)} async-done(((f32[6,512,512]{2,1,0:T(8,128)}), f32[6,32,512]{2,1,0:T(8,128)}) %reduce-scatter.14.cloned.1.call-update) | async-done | bytes 393232 | tf_op jit(solution)/shard_map/reduce_scatter | solution.py:228
  (239 shorter events, 309.1 us)
Async XLA Ops:
  7.2 246.0 %copy-start = (bf16[768,1536]{1,0:T(8,128)(2,1)S(1)}, bf16[768,1536]{1,0:T(8,128)(2,1)}, u32[]{:S(2)}) copy-start(bf16[768,1536]{1,0:T(8,128)(2,1)} %param.35) | copy-start | bytes 7077892
  7.2 32.3 %all-gather.6.cloned.1.call-start = ((), (), s32[]{:S(2)}) async-start(), calls=%async_computation.5 | async-start | bytes 2359296 | tf_op jit(solution)/shard_map/all_gather | solution.py:69
  8.0 79.9 %all-gather.8.cloned.1.call-start = ((), (), s32[]{:S(2)}) async-start(), calls=%async_computation.6 | async-start | bytes 3342336 | tf_op jit(solution)/shard_map/all_gather | solution.py:66
  10.0 211.6 %reduce-scatter.6.cloned.1.call-start = ((), (), s32[]{:S(2)}) async-start(), calls=%async_computation.7 | async-start | bytes 4718592 | tf_op jit(solution)/shard_map/reduce_scatter | solution.py:108
  174.9 46.7 %copy-start.42 = (f32[768]{0:T(1024)S(1)}, f32[768]{0:T(1024)}, u32[]{:S(2)}) copy-start(f32[768]{0:T(1024)} %param.32) | copy-start | bytes 9220
  179.7 45.0 %copy-start.31 = (f32[768]{0:T(1024)S(1)}, f32[768]{0:T(1024)}, u32[]{:S(2)}) copy-start(f32[768]{0:T(1024)} %param.33) | copy-start | bytes 9220
  179.7 45.0 %copy-start.37 = (f32[768]{0:T(1024)S(1)}, f32[768]{0:T(1024)}, u32[]{:S(2)}) copy-start(f32[768]{0:T(1024)} %param.34) | copy-start | bytes 9220
  179.7 73.5 %copy-start.49 = (f32[1536]{0:T(1024)S(1)}, f32[1536]{0:T(1024)}, u32[]{:S(2)}) copy-start(f32[1536]{0:T(1024)} %param.36) | copy-start | bytes 18436
  179.7 73.5 %all-gather.10.cloned.1.call-start = ((), (), s32[]{:S(2)}) async-start(), calls=%async_computation.8 | async-start | bytes 2359296 | tf_op jit(solution)/shard_map/all_gather | solution.py:117
  225.9 95.6 %reduce-scatter.8.cloned.1.call-start = ((), (), s32[]{:S(2)}) async-start(), calls=%async_computation.9 | async-start | bytes 4718592 | tf_op jit(solution)/shard_map/reduce_scatter | solution.py:122
  273.6 47.9 %copy-start.43 = (f32[768]{0:T(1024)S(1)}, f32[768]{0:T(1024)}, u32[]{:S(2)}) copy-start(f32[768]{0:T(1024)} %param.38) | copy-start | bytes 9220
  277.9 46.5 %copy-start.32 = (f32[768]{0:T(1024)S(1)}, f32[768]{0:T(1024)}, u32[]{:S(2)}) copy-start(f32[768]{0:T(1024)} %param.39) | copy-start | bytes 9220
  277.9 47.9 %copy-start.41 = (f32[768]{0:T(1024)S(1)}, f32[768]{0:T(1024)}, u32[]{:S(2)}) copy-start(f32[768]{0:T(1024)} %param.40) | copy-start | bytes 9220
  277.9 79.6 %all-gather.12.cloned.1.call-start = ((), (), s32[]{:S(2)}) async-start(), calls=%async_computation.10 | async-start | bytes 2359296 | tf_op jit(solution)/shard_map/all_gather | solution.py:133
  330.2 87.7 %reduce-scatter.10.cloned.1.call-start = ((), (), s32[]{:S(2)}) async-start(), calls=%async_computation.11 | async-start | bytes 4718592 | tf_op jit(solution)/shard_map/reduce_scatter | solution.py:146
  374.3 47.4 %copy-start.5 = (f32[512,768]{1,0:T(8,128)S(1)}, f32[512,768]{1,0:T(8,128)}, u32[]{:S(2)}) copy-start(f32[512,768]{1,0:T(8,128)} %copy-done.4) | copy-start | bytes 4718596
  374.3 78.0 %all-gather.14.cloned.1.call-start = ((), (), s32[]{:S(2)}) async-start(), calls=%async_computation.12 | async-start | bytes 2359296 | tf_op jit(solution)/shard_map/all_gather | solution.py:156
  424.9 465.4 %reduce-scatter.12.cloned.1.call-start = ((), (), s32[]{:S(2)}) async-start(), calls=%async_computation.13 | async-start | bytes 2359296 | tf_op jit(solution)/shard_map/reduce_scatter | solution.py:219
  766.4 289.9 %all-reduce.5.cloned.1.call-start = ((), (), s32[]{:S(2)}) async-start(), calls=%async_computation.15 | async-start | bytes 28311552 | tf_op jit(solution)/shard_map/psum | solution.py:242
  784.4 105.9 %copy-start.11 = (f32[512,768]{1,0:T(8,128)S(1)}, f32[512,768]{1,0:T(8,128)}, u32[]{:S(2)}) copy-start(f32[512,768]{1,0:T(8,128)} %copy-done.10) | copy-start | bytes 4718596
  784.4 361.1 %reduce-scatter.14.cloned.1.call-start = ((), (), s32[]{:S(2)}) async-start(), calls=%async_computation.14 | async-start | bytes 6684672 | tf_op jit(solution)/shard_map/reduce_scatter | solution.py:228
  890.4 255.2 %copy-start.22 = (f32[6,32,512]{2,1,0:T(8,128)S(1)}, f32[6,32,512]{2,1,0:T(8,128)}, u32[]{:S(2)}) copy-start(f32[6,32,512]{2,1,0:T(8,128)} %param.41) | copy-start | bytes 1179652
  890.4 255.2 %copy-start.23 = (f32[6,32,512]{2,1,0:T(8,128)S(1)}, f32[6,32,512]{2,1,0:T(8,128)}, u32[]{:S(2)}) copy-start(f32[6,32,512]{2,1,0:T(8,128)} %param.42) | copy-start | bytes 1179652
  1056.3 91.1 %copy-start.24 = (f32[384,768]{1,0:T(8,128)S(1)}, f32[384,768]{1,0:T(8,128)}, u32[]{:S(2)}) copy-start(f32[384,768]{1,0:T(8,128)} %get-tuple-element.561) | copy-start | bytes 3538948
  (47 other events, 350.6 us)
Sparse Core Ops, SparseCore 0:
  9.6 29.8 all-gather.5
  42.3 45.4 all-gather.7
  179.8 41.7 reduce-scatter.5
  226.0 27.1 all-gather.9
  278.0 43.3 reduce-scatter.7
  330.3 27.1 all-gather.11
  374.4 43.4 reduce-scatter.9
  425.0 27.1 all-gather.13
  766.5 26.1 reduce-scatter.11
  798.3 258.0 all-reduce.4
  1060.3 85.1 reduce-scatter.13
where the time goes:
time: 1170 us; the launch traced here: 1160 us
  waiting for transfers between devices  519 us (44%)
  matrix products  227 us (19%)
  local copies, waits for them, and re-layouts  200 us (17%)
  blocking collectives  105 us (9%)
  other arithmetic  95.9 us (8%)
  between operations  15.2 us (1%)
    psum x1, waiting for transfers between devices, on_device(): lax.psum((query_weight_grad, key_weight_grad, value_weight_grad, proj_wei...  164 us
    reduce_scatter x1, waiting for transfers between devices, on_device(): lax.psum_scatter(mask_total, 'dp', scatter_dimension=1, tiled=True)  82.3 us
    psum x1, blocking collectives, on_device(): lax.psum((query_weight_grad, key_weight_grad, value_weight_grad, proj_wei...  63.8 us
    mul x4, local copies, waits for them, and re-layouts, apply_mask(): softmax_out.reshape(local_heads, window, blocks, window)  55.4 us
    dot_general x2, matrix products, attend_back(): jnp.einsum('hqk,qhd->khd', grad_scores, query_block, preferred_element_ty...  51.1 us
    mul x4, local copies, waits for them, and re-layouts, attend_back(): grad_tiles * trainable_focus_filter[:, :, None, :]  50.1 us
    dot_general x2, matrix products, attend_back(): jnp.einsum('hqk,khd->qhd', grad_scores, key_rows, preferred_element_type=...  49.5 us
    reduce_sum x2, other arithmetic, attend_back(): jnp.sum(grad_tiles * softmax_out.reshape(local_heads, window, blocks, win...  44.8 us
  transfers between devices with their start and end apart: 11, of which 10 were waited for; matrix products, arithmetic and copies ran while one was open for 4% of the time, Pallas kernels for 0%

commit v1 on v0

v1 whole, which is shorter than its diff:
```python
import functools
import math

import jax
import jax.numpy as jnp
from jax import lax
from jax.experimental import pallas as pl
from jax.experimental.pallas import tpu as pltpu
from jax.sharding import PartitionSpec as P

HEAD_DIM = 64
PAIR = 128


def dot(a, b, dims=(((1,), (0,)), ((), ()))):
    return lax.dot_general(a, b, dims, preferred_element_type=jnp.float32)


NT = (((1,), (1,)), ((), ()))
TN = (((0,), (0,)), ((), ()))


def head_lanes(shape, head):
    lane = lax.broadcasted_iota(jnp.int32, shape, 1)
    return (lane < HEAD_DIM) if head == 0 else (lane >= HEAD_DIM)


def masked_pair(query, key, bias, head):
    own = head_lanes(query.shape, head)
    lane = lax.broadcasted_iota(jnp.int32, query.shape, 1)
    spare = HEAD_DIM if head == 0 else 0
    one = jnp.where(lane == spare, 1.0, 0.0).astype(query.dtype)
    query_head = jnp.where(own, query, one)
    lane_k = lax.broadcasted_iota(jnp.int32, key.shape, 1)
    key_head = jnp.where(
        head_lanes(key.shape, head), key, jnp.where(lane_k == spare, bias, jnp.zeros_like(bias))
    )
    return query_head, key_head


def attend_kernel(factor, q_ref, k_ref, v_ref, bias_ref, dam_ref, ctx_ref, lse_ref):
    query, key, value, bias = q_ref[...], k_ref[...], v_ref[...], bias_ref[...]
    window = dam_ref.shape[2]
    blocks = key.shape[0] // window
    outs, logs = [], []
    for head in range(2):
        query_head, key_head = masked_pair(query, key, bias, head)
        raw = dot(query_head, key_head, NT)
        top = jnp.max(raw, axis=1, keepdims=True)
        exponent = jnp.exp2((raw - top) * factor)
        total = jnp.sum(exponent, axis=1, keepdims=True)
        low = exponent.astype(jnp.bfloat16)
        dam = dam_ref[head]
        acc = None
        for j in range(blocks):
            cols = slice(j * window, (j + 1) * window)
            part = dot(low[:, cols] * dam, value[cols])
            acc = part if acc is None else acc + part
        outs.append(acc * (1.0 / total))
        logs.append(top * factor + jnp.log2(total))
    first = head_lanes(outs[0].shape, 0)
    ctx_ref[...] = jnp.where(first, outs[0], outs[1]).astype(ctx_ref.dtype)
    lse_ref[...] = jnp.where(first, logs[0], logs[1])


def attend(joint, bias, dam, chunk, chunks):
    seq = joint.shape[0]
    width = joint.shape[1] // 3
    window = dam.shape[2]
    halves = seq // window
    pairs = width // PAIR
    tile = window // chunks
    factor = math.log2(math.e) / math.sqrt(HEAD_DIM)
    own = pl.BlockSpec((tile, PAIR), lambda p, b: (b, p))
    rows = halves * tile
    return pl.pallas_call(
        functools.partial(attend_kernel, factor),
        grid=(pairs, halves),
        in_specs=[
            pl.BlockSpec((tile, PAIR), lambda p, b: (b * chunks + chunk, p)),
            pl.BlockSpec((seq, PAIR), lambda p, b: (0, pairs + p)),
            pl.BlockSpec((seq, PAIR), lambda p, b: (0, 2 * pairs + p)),
            pl.BlockSpec((seq, PAIR), lambda p, b: (0, 0)),
            pl.BlockSpec((2, tile, window), lambda p, b: (p, chunk, 0)),
        ],
        out_specs=[own, own],
        out_shape=[
            jax.ShapeDtypeStruct((rows, width), jnp.bfloat16),
            jax.ShapeDtypeStruct((rows, width), jnp.float32),
        ],
        compiler_params=pltpu.CompilerParams(vmem_limit_bytes=40 << 20),
        cost_estimate=pl.CostEstimate(
            flops=16 * rows * seq * width,
            bytes_accessed=rows * width * 8 + seq * width * 4 + 4 * rows * window * pairs,
            transcendentals=rows * seq * width // HEAD_DIM,
        ),
        name="attend",
    )(joint, joint, joint, bias, dam)


def back_kernel(factor, scale, q_ref, k_ref, v_ref, bias_ref, dam_ref, ctx_ref, lse_ref, do_ref,
                dq_ref, dk_ref, dv_ref, gm_ref, dk_acc, dv_acc, gm_acc):
    tile_id, block_id = pl.program_id(1), pl.program_id(2)
    blocks = pl.num_programs(2)
    query, key, value, bias = q_ref[...], k_ref[...], v_ref[...], bias_ref[...]
    up = do_ref[...]
    window = dam_ref.shape[2]
    parts = key.shape[0] // window
    start = jnp.logical_and(tile_id == 0, block_id == 0)

    @pl.when(start)
    def _():
        dk_acc[...] = jnp.zeros_like(dk_acc)
        dv_acc[...] = jnp.zeros_like(dv_acc)

    @pl.when(block_id == 0)
    def _():
        gm_acc[...] = jnp.zeros_like(gm_acc)

    query_t = query.T
    up_t = up.T
    product = up.astype(jnp.float32) * ctx_ref[...].astype(jnp.float32)
    grads = []
    for head in range(2):
        own = head_lanes(query.shape, head)
        rows = slice(head * HEAD_DIM, (head + 1) * HEAD_DIM)
        query_head, key_head = masked_pair(query, key, bias, head)
        up_head = jnp.where(own, up, jnp.zeros_like(up))
        log_total = lse_ref[:, head * HEAD_DIM : head * HEAD_DIM + 1]
        delta = jnp.sum(jnp.where(own, product, 0.0), axis=1, keepdims=True)
        dam = dam_ref[head].astype(jnp.float32)
        raw = dot(query_head, key_head, NT)
        weighted_grad = dot(up_head, value, NT)
        grad_query = None
        for j in range(parts):
            cols = slice(j * window, (j + 1) * window)
            probs = jnp.exp2(raw[:, cols] * factor - log_total)
            gw = weighted_grad[:, cols]
            gm_acc[head] += probs * gw
            dv_acc[rows, cols] += dot(up_t[rows], (probs * dam).astype(jnp.bfloat16))
            ds = (probs * (gw * dam - delta)).astype(jnp.bfloat16)
            dk_acc[rows, cols] += dot(query_t[rows], ds)
            part = dot(ds, key[cols])
            grad_query = part if grad_query is None else grad_query + part
        grads.append(grad_query)
    dq_ref[...] = (jnp.where(head_lanes(query.shape, 0), grads[0], grads[1]) * scale).astype(dq_ref.dtype)

    @pl.when(block_id == blocks - 1)
    def _():
        gm_ref[...] = gm_acc[...].astype(gm_ref.dtype)

    @pl.when(jnp.logical_and(tile_id == pl.num_programs(1) - 1, block_id == blocks - 1))
    def _():
        dk_ref[...] = (dk_acc[...] * scale).T.astype(dk_ref.dtype)
        dv_ref[...] = dv_acc[...].T.astype(dv_ref.dtype)


def attend_back(joint, bias, dam, context, logs, grad_context, chunks):
    seq = joint.shape[0]
    width = joint.shape[1] // 3
    heads, _, window = dam.shape
    pairs = width // PAIR
    tile = window // chunks
    blocks = seq // window
    scale = 1.0 / math.sqrt(HEAD_DIM)
    factor = math.log2(math.e) * scale
    whole = pl.BlockSpec((seq, PAIR), lambda p, a, b: (0, p))
    natural = pl.BlockSpec((tile, PAIR), lambda p, a, b: (b * chunks + a, p))
    chunked = pl.BlockSpec((tile, PAIR), lambda p, a, b: (a * blocks + b, p))
    table = pl.BlockSpec((2, tile, window), lambda p, a, b: (p, a, 0))
    out = jax.ShapeDtypeStruct((seq, width), jnp.bfloat16)
    return pl.pallas_call(
        functools.partial(back_kernel, factor, scale),
        grid=(pairs, chunks, blocks),
        in_specs=[
            natural,
            pl.BlockSpec((seq, PAIR), lambda p, a, b: (0, pairs + p)),
            pl.BlockSpec((seq, PAIR), lambda p, a, b: (0, 2 * pairs + p)),
            pl.BlockSpec((seq, PAIR), lambda p, a, b: (0, 0)),
            table,
            chunked,
            chunked,
            chunked,
        ],
        out_specs=[natural, whole, whole, table],
        out_shape=[out, out, out, jax.ShapeDtypeStruct(dam.shape, jnp.bfloat16)],
        scratch_shapes=[
            pltpu.VMEM((PAIR, seq), jnp.float32),
            pltpu.VMEM((PAIR, seq), jnp.float32),
            pltpu.VMEM((2, tile, window), jnp.float32),
        ],
        compiler_params=pltpu.CompilerParams(vmem_limit_bytes=40 << 20),
        cost_estimate=pl.CostEstimate(
            flops=40 * seq * seq * width,
            bytes_accessed=seq * width * 20 + heads * window * window * 4,
            transcendentals=seq * seq * width // HEAD_DIM,
        ),
        name="attend_back",
    )(joint, joint, joint, bias, dam, context, logs, grad_context)


CHUNKS = 2
softening_heat = 0.5
epsilon = 1e-05


def swap(values):
    return lax.ppermute(values, "tensor", [(0, 1), (1, 0)])


def exchange(partial):
    half = partial.shape[0] // 2
    sent = jnp.concatenate([partial[half:], partial[:half]], axis=0).astype(jnp.bfloat16)
    return partial + swap(sent).astype(jnp.float32)


def layer_norm(values):
    centre = values - jnp.mean(values, axis=-1, keepdims=True)
    spread = jnp.mean(centre * centre, axis=-1, keepdims=True)
    inverse = lax.rsqrt(spread + epsilon)
    return centre * inverse, inverse


def norm_back(upstream, normal, inverse, gain):
    scaled = upstream * gain
    first_mean = jnp.mean(scaled, axis=-1, keepdims=True)
    second_mean = jnp.mean(scaled * normal, axis=-1, keepdims=True)
    return inverse * (scaled - first_mean - normal * second_mean)


def on_device(
    inputs, lengths, query_weight, query_bias, key_weight, value_weight, value_bias,
    proj_weight, proj_bias, attn_gain, attn_shift, up_weight, up_bias, down_weight,
    down_bias, ffn_gain, ffn_shift, filter_couple_scores, filter_smoothing_jitter, cotangent,
):
    half = inputs.shape[0]
    width = query_weight.shape[1]
    step = half // CHUNKS
    low = jnp.bfloat16
    full = jnp.float32
    place = lax.axis_index("tensor")
    softened = jax.nn.sigmoid((filter_couple_scores + filter_smoothing_jitter) / softening_heat)
    dam = lax.all_gather(softened.astype(low), "dp", axis=1, tiled=True)
    others = swap(inputs)
    other_cotangent = swap(cotangent)
    ids = jnp.arange(half, dtype=jnp.int32)
    slots = jnp.concatenate([ids + place * half, ids + (1 - place) * half])
    live = slots < lengths[0]
    bias = jnp.broadcast_to(jnp.where(live, 0.0, -1e30).astype(low)[:, None], (2 * half, PAIR))
    rows = jnp.concatenate([inputs, others], axis=0)
    joint_weight = jnp.concatenate([query_weight, key_weight, value_weight], axis=1)
    joint_bias = jnp.concatenate([query_bias, jnp.zeros_like(query_bias), value_bias])
    joint = (dot(rows, joint_weight) + joint_bias).astype(low)

    def pick(own, other, c):
        part = slice(c * step, (c + 1) * step)
        return jnp.concatenate([own[part], other[part]], axis=0)

    contexts, logs, sums = [], [], []
    for c in range(CHUNKS):
        context, log_total = attend(joint, bias, dam, c, CHUNKS)
        contexts.append(context)
        logs.append(log_total)
        sums.append(exchange(dot(context, proj_weight)))
    small = {}

    def count(name, values):
        small[name] = small.get(name, 0.0) + values

    root = math.sqrt(0.5)
    saved = []
    for c in range(CHUNKS):
        pre = pick(inputs, others, c).astype(full) + sums[c] + proj_bias
        normal, inverse = layer_norm(pre)
        normed = normal * attn_gain + attn_shift
        hidden = normed.astype(low)
        upper = dot(hidden, up_weight) + up_bias
        phi = 0.5 * (1.0 + lax.erf(upper * root))
        active = (upper * phi).astype(low)
        slope = (phi + upper * jnp.exp(-0.5 * upper * upper) * (1.0 / math.sqrt(2.0 * math.pi))).astype(low)
        summed = exchange(dot(active, down_weight))
        saved.append((normal, inverse, normed, hidden, active, slope, summed))
    outputs, backs = [], []
    down_grad = up_grad = None
    for c in range(CHUNKS):
        normal, inverse, normed, hidden, active, slope, summed = saved[c]
        normal_ffn, inverse_ffn = layer_norm(normed + summed + down_bias)
        outputs.append((normal_ffn[:step] * ffn_gain + ffn_shift).astype(low))
        alive = jnp.concatenate(
            [live[c * step : (c + 1) * step], live[half + c * step : half + (c + 1) * step]]
        )
        grad_out = pick(cotangent, other_cotangent, c).astype(full) * alive[:, None].astype(full)
        grad_ffn = norm_back(grad_out, normal_ffn, inverse_ffn, ffn_gain)
        count("ffn_gain", jnp.sum(grad_out[:step] * normal_ffn[:step], axis=0))
        count("ffn_shift", jnp.sum(grad_out[:step], axis=0))
        count("down_bias", jnp.sum(grad_ffn[:step], axis=0))
        grad_low = grad_ffn.astype(low)
        grad_upper = (dot(grad_low, down_weight, NT) * slope.astype(full)).astype(low)
        grad_hidden = exchange(dot(grad_upper, up_weight, NT))
        backs.append((grad_ffn, grad_hidden))
        count("up_bias", jnp.sum(grad_upper.astype(full), axis=0))
        part = dot(active, grad_low, TN)
        down_grad = part if down_grad is None else down_grad + part
        part = dot(hidden, grad_upper, TN)
        up_grad = part if up_grad is None else up_grad + part
    up_sum, down_sum = lax.psum((up_grad.astype(low), down_grad.astype(low)), "dp")
    grads_attn, grads_low = [], []
    proj_grad = None
    for c in range(CHUNKS):
        normal, inverse = saved[c][0], saved[c][1]
        grad_ffn, grad_hidden = backs[c]
        grad_normed = grad_ffn + grad_hidden
        grad_attn = norm_back(grad_normed, normal, inverse, attn_gain)
        count("attn_gain", jnp.sum(grad_normed[:step] * normal[:step], axis=0))
        count("attn_shift", jnp.sum(grad_normed[:step], axis=0))
        count("proj_bias", jnp.sum(grad_attn[:step], axis=0))
        grads_attn.append(grad_attn[:step])
        grad_low = grad_attn.astype(low)
        grads_low.append(dot(grad_low, proj_weight, NT).astype(low))
        part = dot(contexts[c], grad_low, TN)
        proj_grad = part if proj_grad is None else proj_grad + part
    grad_context = jnp.concatenate(grads_low, axis=0)
    grad_query, grad_key, grad_value, mask_grad = attend_back(
        joint, bias, dam, jnp.concatenate(contexts, axis=0), jnp.concatenate(logs, axis=0), grad_context, CHUNKS
    )
    mask_sum = lax.psum_scatter(mask_grad, "dp", scatter_dimension=1, tiled=True)
    mask_out = mask_sum.astype(full) * softened * (1.0 - softened) / softening_heat

    def back_rows(part):
        return (
            dot(grad_query[part], query_weight, NT)
            + dot(grad_key[part], key_weight, NT)
            + dot(grad_value[part], value_weight, NT)
        )

    arrived = swap(back_rows(slice(half, None)).astype(low))
    input_grad = (jnp.concatenate(grads_attn, axis=0) + back_rows(slice(0, half)) + arrived.astype(full)).astype(low)
    query_grad = dot(rows, grad_query, TN)
    key_grad = dot(rows, grad_key, TN)
    value_grad = dot(rows, grad_value, TN)
    query_bias_grad = jnp.sum(grad_query.astype(full), axis=0)
    value_bias_grad = jnp.sum(grad_value.astype(full), axis=0)
    model = inputs.shape[1]
    joined = jnp.concatenate(
        [query_bias_grad, value_bias_grad, small["up_bias"]]
        + [small[n] for n in ("proj_bias", "down_bias", "attn_gain", "attn_shift", "ffn_gain", "ffn_shift")]
    )
    table = joined.reshape(-1, model)
    extra = -table.shape[0] % 16
    table = jnp.concatenate([table, jnp.zeros((extra, model), full)], axis=0)
    proj_table = jnp.concatenate([proj_grad, table], axis=0).astype(low)
    tail = (query_grad.astype(low), key_grad.astype(low), value_grad.astype(low), proj_table)
    tail, up_sum, down_sum = lax.optimization_barrier((tail, up_sum, down_sum))
    query_sum, key_sum, value_sum, proj_table = lax.psum(tail, "dp")
    flat = proj_table[width:].astype(full).reshape(-1)
    spread = flat[2 * width + up_bias.shape[0] :][: 6 * model].reshape(6, model)
    spread = spread + swap(spread)
    return (
        jnp.concatenate(outputs, axis=0),
        input_grad,
        query_sum.astype(full),
        key_sum.astype(full),
        value_sum.astype(full),
        proj_table[:width].astype(full),
        up_sum.astype(full),
        down_sum.astype(full),
        flat[:width],
        flat[width : 2 * width],
        flat[2 * width :][: up_bias.shape[0]],
        spread[0],
        spread[1],
        spread[2],
        spread[3],
        spread[4],
        spread[5],
        mask_out,
    )


def solution(mesh):
    in_specs = (
        P(("dp", "tensor"), None),
        P("dp"),
        P(None, "tensor"),
        P("tensor"),
        P(None, "tensor"),
        P(None, "tensor"),
        P("tensor"),
        P("tensor", None),
        P(),
        P(),
        P(),
        P(None, "tensor"),
        P("tensor"),
        P("tensor", None),
        P(),
        P(),
        P(),
        P("tensor", "dp", None),
        P("tensor", "dp", None),
        P(("dp", "tensor"), None),
    )
    out_specs = (
        P(("dp", "tensor"), None),
        P(("dp", "tensor"), None),
        P(None, "tensor"),
        P(None, "tensor"),
        P(None, "tensor"),
        P("tensor", None),
        P(None, "tensor"),
        P("tensor", None),
        P("tensor"),
        P("tensor"),
        P("tensor"),
        P(),
        P(),
        P(),
        P(),
        P(),
        P(),
        P("tensor", "dp", None),
    )
    return jax.shard_map(
        on_device, mesh=mesh, in_specs=in_specs, out_specs=out_specs, check_vma=False
    )
```

time: 1170 us -> 488 us (0.42)
  waiting for transfers between devices: 519 us -> 295 us
  matrix products: 227 us -> 44.6 us
  local copies, waits for them, and re-layouts: 200 us -> 25.8 us
  blocking collectives: 105 us -> 0 us
  other arithmetic: 95.9 us -> 45.2 us
  Pallas kernels: 0 us -> 42.8 us
  starting transfers between devices: 0.45 us -> 13 us
    dot_general x26 -> x28, matrix products: 227 us -> 44.6 us  [dot(): return lax.dot_general(a, b, dims, preferred_element_type=jnp.float32)]
    reduce_scatter x5 -> x1, waiting for transfers between devices: 211 us -> 59.8 us  [on_device(): lax.psum_scatter(mask_grad, 'dp', scatter_dimension=1, tiled=True)]
    mul x10 -> x0, local copies, waits for them, and re-layouts: 139 us -> none  [the longest x4 55.4 us: apply_mask(): softmax_out.reshape(local_heads, window, blocks, window)]
    all_gather x5 -> x1, waiting for transfers between devices: 144 us -> 21.7 us  [on_device(): dam = lax.all_gather(softened.astype(low), 'dp', axis=1, tiled=True)]
    psum x2 -> x0, blocking collectives: 105 us -> none  [the longest x1 63.8 us: on_device(): lax.psum((query_weight_grad, key_weight_grad, value_weight_grad, proj_wei...]
    ppermute x0 -> x10, waiting for transfers between devices: none -> 102 us  [swap(): return lax.ppermute(values, 'tensor', [(0, 1), (1, 0)])]
    psum x1 -> x2, waiting for transfers between devices: 164 us -> 111 us  [the longest x1 74.8 us: on_device(): query_sum, key_sum, value_sum, proj_table = lax.psum(tail, 'dp')]
    reduce_sum x10 -> x12, other arithmetic: 59.8 us -> 13.8 us  [the longest x2 6.79 us: norm_back(): first_mean = jnp.mean(scaled, axis=-1, keepdims=True)]
  transfers between devices with their start and end apart: 11 -> 14, of which waited for: 10 -> 12; matrix products, arithmetic and copies ran while one was open for 4% -> 16% of each run, Pallas kernels for 0% -> 9%
where the time goes in v1:
time: 488 us; the launch traced here: 482 us
  waiting for transfers between devices  295 us (60%)
  other arithmetic  45.2 us (9%)
  matrix products  44.6 us (9%)
  Pallas kernels  42.8 us (9%)
  local copies, waits for them, and re-layouts  25.8 us (5%)
  between operations  15.8 us (3%)
  starting transfers between devices  13 us (3%)
    ppermute x10, waiting for transfers between devices, swap(): return lax.ppermute(values, 'tensor', [(0, 1), (1, 0)])  102 us
    psum x1, waiting for transfers between devices, on_device(): query_sum, key_sum, value_sum, proj_table = lax.psum(tail, 'dp')  74.8 us
    reduce_scatter x1, waiting for transfers between devices, on_device(): lax.psum_scatter(mask_grad, 'dp', scatter_dimension=1, tiled=True)  59.8 us
    dot_general x28, matrix products, dot(): return lax.dot_general(a, b, dims, preferred_element_type=jnp.float32)  44.6 us
    psum x1, waiting for transfers between devices, on_device(): lax.psum((up_grad.astype(low), down_grad.astype(low)), 'dp')  36.4 us
    pallas_call x1, Pallas kernels, attend_back(): pl.pallas_call(functools.partial(back_kernel, factor, scale), grid=(pairs...  26.9 us
    all_gather x1, waiting for transfers between devices, on_device(): dam = lax.all_gather(softened.astype(low), 'dp', axis=1, tiled=True)  21.7 us
    unnamed x137, local copies, waits for them, and re-layouts  18.3 us
  transfers between devices with their start and end apart: 14, of which 12 were waited for; matrix products, arithmetic and copies ran while one was open for 16% of the time, Pallas kernels for 9%

profile of v1, /device:TPU:0, one launch (start us, length us, event | category | flops | bytes accessed | tf_op | source)
XLA Modules:
  0.0 482.4 jit_solution(12829829431353002651)
XLA Ops:
  9.4 3.1 collective-permute-start
  14.1 17.1 %collective-permute-done = bf16[512,768]{1,0:T(8,128)(2,1)} collective-permute-done((bf16[512,768]{1,0:T(8,128)(2,1)}, bf16[512,768]{1,0:T(8,128)(2,1)}, u32[]{:S(2)}, u32[]{:S(2)}) %collective-permute-start) | collective-permute-done | bytes 786464 | tf_op jit(solution)/shard_map/ppermute | solution.py:208
  33.6 3.6 add_convert_fusion.2.q_ref.k_ref.v_ref
  37.2 21.7 %all-gather.2.cloned.1.call-done.dam_ref = bf16[6,512,512]{2,1,0:T(8,128)(2,1)} async-done(((bf16[6,32,512]{2,1,0:T(8,128)(2,1)}), bf16[6,512,512]{2,1,0:T(8,128)(2,1)}) %all-gather.2.cloned.1.call-update) | async-done | bytes 3145744 | tf_op jit(solution)/shard_map/all_gather | solution.py:243
  62.6 7.9 %attend.2 = (bf16[512,384]{1,0:T(8,128)(2,1)S(1)}, f32[512,384]{1,0:T(8,128)S(1)}) custom-call(bf16[1024,1152]{1,0:T(8,128)(2,1)S(1)} %copy-done.15, bf16[1024,1152]{1,0:T(8,128)(2,1)S(1)} %copy-done.15, bf16[1024,1152]{1,0:T(8,128)(2,1)S(1)} %copy-done.15, bf16[1024,128]{1,0:T(8,128)(2,1)S(1)} %broadcast_in_dim.17.bias_ref, bf16[6,512,512]{2,1,0:T(8,128)(2,1)S(1)} %copy-done.13), custom_call_target="tpu_custom_call" | custom-call | flops 3221225472 | bytes 6291456 | tf_op jit(solution)/shard_map/attend/pallas_call | solution.py:76
  74.7 8.1 %attend.3 = (bf16[512,384]{1,0:T(8,128)(2,1)S(1)}, f32[512,384]{1,0:T(8,128)S(1)}) custom-call(bf16[1024,1152]{1,0:T(8,128)(2,1)S(1)} %copy-done.15, bf16[1024,1152]{1,0:T(8,128)(2,1)S(1)} %copy-done.15, bf16[1024,1152]{1,0:T(8,128)(2,1)S(1)} %copy-done.15, bf16[1024,128]{1,0:T(8,128)(2,1)S(1)} %broadcast_in_dim.17.bias_ref, bf16[6,512,512]{2,1,0:T(8,128)(2,1)S(1)} %copy-done.13), custom_call_target="tpu_custom_call" | custom-call | flops 3221225472 | bytes 6291456 | tf_op jit(solution)/shard_map/attend/pallas_call | solution.py:76
  88.7 5.3 %collective-permute-done.1 = bf16[512,768]{1,0:T(8,128)(2,1)} collective-permute-done((bf16[512,768]{1,0:T(8,128)(2,1)}, bf16[512,768]{1,0:T(8,128)(2,1)}, u32[]{:S(2)}, u32[]{:S(2)}) %collective-permute-start.1) | collective-permute-done | bytes 786464 | tf_op jit(solution)/shard_map/ppermute | solution.py:208
  94.0 16.1 %collective-permute-done.3 = bf16[512,768]{1,0:T(8,128)(2,1)} collective-permute-done((bf16[512,768]{1,0:T(8,128)(2,1)}, bf16[512,768]{1,0:T(8,128)(2,1)}, u32[]{:S(2)}, u32[]{:S(2)}) %collective-permute-start.3) | collective-permute-done | bytes 786464 | tf_op jit(solution)/shard_map/ppermute | solution.py:208
  127.0 11.3 %collective-permute-done.2 = bf16[512,768]{1,0:T(8,128)(2,1)S(1)} collective-permute-done((bf16[512,768]{1,0:T(8,128)(2,1)S(1)}, bf16[512,768]{1,0:T(8,128)(2,1)S(1)}, u32[]{:S(2)}, u32[]{:S(2)}) %collective-permute-start.2) | collective-permute-done | bytes 786464 | tf_op jit(solution)/shard_map/ppermute | solution.py:208
  138.2 15.3 %collective-permute-done.4 = bf16[512,768]{1,0:T(8,128)(2,1)S(1)} collective-permute-done((bf16[512,768]{1,0:T(8,128)(2,1)S(1)}, bf16[512,768]{1,0:T(8,128)(2,1)S(1)}, u32[]{:S(2)}, u32[]{:S(2)}) %collective-permute-start.4) | collective-permute-done | bytes 786464 | tf_op jit(solution)/shard_map/ppermute | solution.py:208
  158.0 2.9 convert_reduce_fusion.1
  167.0 2.7 convert_reduce_fusion
  174.0 2.6 fusion.72
  178.2 2.8 add_convert_fusion.1
  181.0 2.9 add_convert_fusion
  185.3 7.9 %collective-permute-done.6 = bf16[512,768]{1,0:T(8,128)(2,1)} collective-permute-done((bf16[512,768]{1,0:T(8,128)(2,1)}, bf16[512,768]{1,0:T(8,128)(2,1)}, u32[]{:S(2)}, u32[]{:S(2)}) %collective-permute-start.6) | collective-permute-done | bytes 786464 | tf_op jit(solution)/shard_map/ppermute | solution.py:208
  193.3 14.3 %collective-permute-done.7 = bf16[512,768]{1,0:T(8,128)(2,1)S(1)} collective-permute-done((bf16[512,768]{1,0:T(8,128)(2,1)}, bf16[512,768]{1,0:T(8,128)(2,1)S(1)}, u32[]{:S(2)}, u32[]{:S(2)}) %collective-permute-start.7) | collective-permute-done | bytes 786464 | tf_op jit(solution)/shard_map/ppermute | solution.py:208
  207.6 4.7 multiply_reduce_fusion.10
  220.5 26.9 %attend_back.1 = (bf16[1024,384]{1,0:T(8,128)(2,1)S(1)}, bf16[1024,384]{1,0:T(8,128)(2,1)S(1)}, bf16[1024,384]{1,0:T(8,128)(2,1)S(1)}, bf16[6,512,512]{2,1,0:T(8,128)(2,1)S(1)}) custom-call(bf16[1024,1152]{1,0:T(8,128)(2,1)S(1)} %copy-done.16, bf16[1024,1152]{1,0:T(8,128)(2,1)S(1)} %copy-done.16, bf16[1024,1152]{1,0:T(8,128)(2,1)S(1)} %copy-done.16, ...), custom_call_target="tpu_custom_call" | custom-call | flops 16106127360 | bytes 14155776 | tf_op jit(solution)/shard_map/attend_back/pallas_call | solution.py:172
  262.9 36.4 %all-reduce.7.cloned.1.call-done = (bf16[768,1536]{1,0:T(8,128)(2,1)}, bf16[1536,768]{1,0:T(8,128)(2,1)}) async-done(((bf16[768,1536]{1,0:T(8,128)(2,1)}, bf16[1536,768]{1,0:T(8,128)(2,1)}), (bf16[768,1536]{1,0:T(8,128)(2,1)}, bf16[1536,768]{1,0:T(8,128)(2,1)})) %all-reduce.7.cloned.1.call-update) | async-done | bytes 4718608 | tf_op jit(solution)/shard_map/psum | solution.py:306
  307.2 14.8 %collective-permute-done.8 = bf16[512,768]{1,0:T(8,128)(2,1)S(1)} collective-permute-done((bf16[512,768]{1,0:T(8,128)(2,1)S(1)}, bf16[512,768]{1,0:T(8,128)(2,1)S(1)}, u32[]{:S(2)}, u32[]{:S(2)}) %collective-permute-start.8) | collective-permute-done | bytes 786464 | tf_op jit(solution)/shard_map/ppermute | solution.py:208
  323.7 2.8 convert_element_type.229
  329.1 74.8 %all-reduce.5.cloned.1.call-done = (bf16[768,384]{1,0:T(8,128)(2,1)}, bf16[768,384]{1,0:T(8,128)(2,1)}, bf16[768,384]{1,0:T(8,128)(2,1)}, bf16[400,768]{1,0:T(8,128)(2,1)}) async-done(((bf16[768,384]{1,0:T(8,128)(2,1)}, bf16[768,384]{1,0:T(8,128)(2,1)}, bf16[768,384]{1,0:T(8,128)(2,1)}, bf16[400,768]{1,0:T(8,128)(2,1)}), (bf16[768,384]{1,0:T(8,128)(2,1)}, bf16[768,384]{1,0:T(8,128)(2,1)}, ...) | async-done | bytes 2383888 | tf_op jit(solution)/shard_map/psum | solution.py:354
  413.7 59.8 %reduce-scatter.2.cloned.1.call-done = bf16[6,32,512]{2,1,0:T(8,128)(2,1)} async-done(((bf16[6,512,512]{2,1,0:T(8,128)(2,1)}), bf16[6,32,512]{2,1,0:T(8,128)(2,1)}) %reduce-scatter.2.cloned.1.call-update) | async-done | bytes 196624 | tf_op jit(solution)/shard_map/reduce_scatter | solution.py:326
  (272 shorter events, 100.7 us)
Async XLA Ops:
  7.2 106.3 %copy-start = (bf16[768,1536]{1,0:T(8,128)(2,1)S(1)}, bf16[768,1536]{1,0:T(8,128)(2,1)}, u32[]{:S(2)}) copy-start(bf16[768,1536]{1,0:T(8,128)(2,1)} %param.31) | copy-start | bytes 7077892
  7.2 51.7 %all-gather.2.cloned.1.call-start = ((), (), s32[]{:S(2)}) async-start(), calls=%async_computation.1 | async-start | bytes 3342336 | tf_op jit(solution)/shard_map/all_gather | solution.py:243
  9.4 289.9 %all-reduce.7.cloned.1.call-start = ((), (), s32[]{:S(2)}) async-start(), calls=%async_computation.4 | async-start | bytes 9437184 | tf_op jit(solution)/shard_map/psum | solution.py:306
  9.4 21.8 %collective-permute-start = (bf16[512,768]{1,0:T(8,128)(2,1)}, bf16[512,768]{1,0:T(8,128)(2,1)}, u32[]{:S(2)}, u32[]{:S(2)}) collective-permute-start(bf16[512,768]{1,0:T(8,128)(2,1)} %param.20), channel_id=1, source_target_pairs={{0,1},{1,0},{2,3},{3,2},{4,5},{5,4},{6,7},{7,6},{8,9},{9,8},{10,11... | collective-permute-start | bytes 2359304 | tf_op jit(solution)/shard_map/ppermute | solution.py:208
  12.5 110.9 %collective-permute-start.5 = (bf16[512,768]{1,0:T(8,128)(2,1)}, bf16[512,768]{1,0:T(8,128)(2,1)}, u32[]{:S(2)}, u32[]{:S(2)}) collective-permute-start(bf16[512,768]{1,0:T(8,128)(2,1)} %param.39), channel_id=1, source_target_pairs={{0,1},{1,0},{2,3},{3,2},{4,5},{5,4},{6,7},{7,6},{8,9},{9,8},{10,11... | collective-permute-start | bytes 2359304 | tf_op jit(solution)/shard_map/ppermute | solution.py:208
  73.3 20.7 %collective-permute-start.1 = (bf16[512,768]{1,0:T(8,128)(2,1)}, bf16[512,768]{1,0:T(8,128)(2,1)}, u32[]{:S(2)}, u32[]{:S(2)}) collective-permute-start(bf16[512,768]{1,0:T(8,128)(2,1)} %pad_maximum_fusion.1), channel_id=1, source_target_pairs={{0,1},{1,0},{2,3},{3,2},{4,5},{5,4},{6,7},{7,6},{8,9},{9,8},{10,11... | collective-permute-start | bytes 2359304 | tf_op jit(solution)/shard_map/ppermute | solution.py:208
  85.5 24.6 %collective-permute-start.3 = (bf16[512,768]{1,0:T(8,128)(2,1)}, bf16[512,768]{1,0:T(8,128)(2,1)}, u32[]{:S(2)}, u32[]{:S(2)}) collective-permute-start(bf16[512,768]{1,0:T(8,128)(2,1)} %pad_maximum_fusion.3), channel_id=1, source_target_pairs={{0,1},{1,0},{2,3},{3,2},{4,5},{5,4},{6,7},{7,6},{8,9},{9,8},{10,11... | collective-permute-start | bytes 2359304 | tf_op jit(solution)/shard_map/ppermute | solution.py:208
  86.2 23.9 %copy-start.33 = (f32[512,768]{1,0:T(8,128)S(1)}, f32[512,768]{1,0:T(8,128)}, u32[]{:S(2)}) copy-start(f32[512,768]{1,0:T(8,128)} %get-tuple-element.137) | copy-start | bytes 4718596
  112.3 41.2 %copy-start.17 = (f32[512,768]{1,0:T(8,128)}, f32[512,768]{1,0:T(8,128)S(1)}, u32[]{:S(2)}) copy-start(f32[512,768]{1,0:T(8,128)S(1)} %get-tuple-element.89) | copy-start | bytes 4718596
  112.3 41.2 %copy-start.19 = (f32[512,768]{1,0:T(8,128)}, f32[512,768]{1,0:T(8,128)S(1)}, u32[]{:S(2)}) copy-start(f32[512,768]{1,0:T(8,128)S(1)} %get-tuple-element.129) | copy-start | bytes 4718596
  113.2 65.0 %copy-start.29 = (f32[512,768]{1,0:T(8,128)}, f32[512,768]{1,0:T(8,128)S(1)}, u32[]{:S(2)}) copy-start(f32[512,768]{1,0:T(8,128)S(1)} %subtract_multiply_fusion.5) | copy-start | bytes 4718596
  114.0 49.5 %copy-start.27 = (f32[512,768]{1,0:T(8,128)}, f32[512,768]{1,0:T(8,128)S(1)}, u32[]{:S(2)}) copy-start(f32[512,768]{1,0:T(8,128)S(1)} %subtract_multiply_fusion.7) | copy-start | bytes 4718596
  117.7 20.5 %collective-permute-start.2 = (bf16[512,768]{1,0:T(8,128)(2,1)S(1)}, bf16[512,768]{1,0:T(8,128)(2,1)S(1)}, u32[]{:S(2)}, u32[]{:S(2)}) collective-permute-start(bf16[512,768]{1,0:T(8,128)(2,1)S(1)} %pad_maximum_fusion.2), channel_id=1, source_target_pairs={{0,1},{1,0},{2,3},{3,2},{4,5},{5,4},{6,7},{7,6},{8,9},{9,8},{10,11... | collective-permute-start | bytes 2359304 | tf_op jit(solution)/shard_map/ppermute | solution.py:208
  122.4 31.1 %collective-permute-start.4 = (bf16[512,768]{1,0:T(8,128)(2,1)S(1)}, bf16[512,768]{1,0:T(8,128)(2,1)S(1)}, u32[]{:S(2)}, u32[]{:S(2)}) collective-permute-start(bf16[512,768]{1,0:T(8,128)(2,1)S(1)} %pad_maximum_fusion.4), channel_id=1, source_target_pairs={{0,1},{1,0},{2,3},{3,2},{4,5},{5,4},{6,7},{7,6},{8,9},{9,8},{10,11... | collective-permute-start | bytes 2359304 | tf_op jit(solution)/shard_map/ppermute | solution.py:208
  125.7 27.8 %copy-start.61 = (f32[768]{0:T(1024)S(1)}, f32[768]{0:T(1024)}, u32[]{:S(2)}) copy-start(f32[768]{0:T(1024)} %param.34) | copy-start | bytes 9220
  172.5 20.7 %collective-permute-start.6 = (bf16[512,768]{1,0:T(8,128)(2,1)}, bf16[512,768]{1,0:T(8,128)(2,1)}, u32[]{:S(2)}, u32[]{:S(2)}) collective-permute-start(bf16[512,768]{1,0:T(8,128)(2,1)} %pad_maximum_fusion.7), channel_id=1, source_target_pairs={{0,1},{1,0},{2,3},{3,2},{4,5},{5,4},{6,7},{7,6},{8,9},{9,8},{10,11... | collective-permute-start | bytes 2359304 | tf_op jit(solution)/shard_map/ppermute | solution.py:208
  177.6 29.9 %collective-permute-start.7 = (bf16[512,768]{1,0:T(8,128)(2,1)}, bf16[512,768]{1,0:T(8,128)(2,1)S(1)}, u32[]{:S(2)}, u32[]{:S(2)}) collective-permute-start(bf16[512,768]{1,0:T(8,128)(2,1)} %pad_maximum_fusion.9), channel_id=1, source_target_pairs={{0,1},{1,0},{2,3},{3,2},{4,5},{5,4},{6,7},{7,6},{8,9},{9,8},{10,11... | collective-permute-start | bytes 2359304 | tf_op jit(solution)/shard_map/ppermute | solution.py:208
  183.9 220.0 %all-reduce.5.cloned.1.call-start = ((), (), s32[]{:S(2)}) async-start(), calls=%async_computation.3 | async-start | bytes 4767744 | tf_op jit(solution)/shard_map/psum | solution.py:354
  299.4 174.2 %reduce-scatter.2.cloned.1.call-start = ((), (), s32[]{:S(2)}) async-start(), calls=%async_computation.2 | async-start | bytes 3342336 | tf_op jit(solution)/shard_map/reduce_scatter | solution.py:326
  303.5 18.5 %collective-permute-start.8 = (bf16[512,768]{1,0:T(8,128)(2,1)S(1)}, bf16[512,768]{1,0:T(8,128)(2,1)S(1)}, u32[]{:S(2)}, u32[]{:S(2)}) collective-permute-start(bf16[512,768]{1,0:T(8,128)(2,1)S(1)} %add_convert_fusion.3), channel_id=1, source_target_pairs={{0,1},{1,0},{2,3},{3,2},{4,5},{5,4},{6,7},{7,6},{8,9},{9,8},{10,11... | collective-permute-start | bytes 2359304 | tf_op jit(solution)/shard_map/ppermute | solution.py:208
  404.7 8.3 %collective-permute-start.9 = (f32[6,768]{1,0:T(8,128)S(1)}, f32[6,768]{1,0:T(8,128)S(1)}, u32[]{:S(2)}, u32[]{:S(2)}) collective-permute-start(f32[6,768]{1,0:T(8,128)S(1)} %slice.280), channel_id=1, source_target_pairs={{0,1},{1,0},{2,3},{3,2},{4,5},{5,4},{6,7},{7,6},{8,9},{9,8},{10,11... | collective-permute-start | bytes 55304 | tf_op jit(solution)/shard_map/ppermute | solution.py:208
  410.9 62.7 %copy-start.46 = (f32[6,32,512]{2,1,0:T(8,128)S(1)}, f32[6,32,512]{2,1,0:T(8,128)}, u32[]{:S(2)}) copy-start(f32[6,32,512]{2,1,0:T(8,128)} %param.37) | copy-start | bytes 1179652
  410.9 62.7 %copy-start.47 = (f32[6,32,512]{2,1,0:T(8,128)S(1)}, f32[6,32,512]{2,1,0:T(8,128)}, u32[]{:S(2)}) copy-start(f32[6,32,512]{2,1,0:T(8,128)} %param.38) | copy-start | bytes 1179652
  411.9 63.4 %copy-start.1 = (bf16[768,1536]{1,0:T(8,128)(2,1)S(1)}, bf16[768,1536]{1,0:T(8,128)(2,1)}, u32[]{:S(2)}) copy-start(bf16[768,1536]{1,0:T(8,128)(2,1)} %param.31) | copy-start | bytes 7077892
  (54 other events, 283.0 us)
Sparse Core Ops, SparseCore 0:
  10.8 48.0 all-gather.1
  184.1 115.2 all-reduce.6
  303.9 99.9 all-reduce.4
  407.6 65.9 reduce-scatter.1
